TPU v7x, 32 devices: a whole 2x2x4 slice. The times are simulated.
32 devices in a mesh: row: 4 (over y, core), col: 8 (over z, x).
Axes of the slice: x: 2, y: 2, z: 4, core: 2. Of those that a mesh axis runs over, the one named last changes fastest.
Arguments:
- matrix: float32 [4096, 4096], P('row', 'col'), may hold values from -12 to 12, as said below
Outputs:
- sign_estimate: float32 [4096, 4096], P('row', 'col')
Inputs may be any that keep to these rules, and one draw needn't show every extreme that they name: `matrix`: symmetric; the magnitudes of its eigenvalues, divided by the root mean square of all its eigenvalues, lie between 0.4 and 1.7.
All inputs are finite; a program needn't handle non-finite values.
Results may differ from a plain program's by a relative error of at most 0.0002.
Values sent between devices are 32-bit elements; how exact they have to be, the bound alone decides.
A program may use at most 64 MiB of HBM per device.

v0:
```python
import jax
import jax.numpy as jnp
from jax import lax
from jax.sharding import PartitionSpec as P

N = 4096
ITERS = 2


def shards(matrix):
    total = lax.psum(jnp.sum(matrix * matrix), ("row", "col"))
    factor = jnp.sqrt(N / total)
    x_iter = matrix * factor
    for step in range(ITERS):
        source = x_iter
        rows_panel = lax.all_gather(source, "col", axis=1, tiled=True)
        cols_panel = lax.all_gather(source, "row", axis=0, tiled=True)
        square = jnp.dot(
            rows_panel,
            cols_panel,
            preferred_element_type=jnp.float32,
            precision=lax.Precision.HIGHEST,
        )
        cube_block = jnp.dot(
            rows_panel,
            lax.all_gather(square, "row", axis=0, tiled=True),
            preferred_element_type=jnp.float32,
            precision=lax.Precision.HIGHEST,
        )
        x_iter = 1.5 * x_iter - 0.5 * cube_block
    return x_iter


def solution(mesh):
    in_specs = (P("row", "col"),)
    out_specs = P("row", "col")
    return jax.shard_map(shards, mesh=mesh, in_specs=in_specs, out_specs=out_specs, check_vma=False)
```

profile of v0, /device:TPU:0, one launch (start us, length us, event | category | flops | bytes accessed | tf_op | source)
XLA Modules:
  0.0 875.6 jit_solution(11313682879477920894)
XLA Ops:
  6.5 2.7 multiply_reduce_fusion
  9.3 42.2 %psum.7 = f32[]{:T(128)} all-reduce(f32[]{:T(128)} %multiply_reduce_fusion), channel_id=1, replica_groups=mesh['row'=4,'col'=8] {'row','col'}, use_global_device_ids=true, to_apply=%region_1.0 | all-reduce | flops 1 | bytes 8 | tf_op jit(solution)/shard_map/psum | solution.py:11
  52.2 3.1 broadcast_multiply_fusion
  55.3 0.0 all-gather.9.cloned.1.call-update
  55.3 0.0 all-gather.7.cloned.1.call-start
  55.4 0.7 all-gather.7.cloned.1.call-update
  56.1 0.0 all-gather.11.cloned.1.call-start
  56.1 57.6 %all-gather.9.cloned.1.call-done = f32[4096,512]{1,0:T(8,128)} async-done(((f32[1024,512]{1,0:T(8,128)}), f32[4096,512]{1,0:T(8,128)}) %all-gather.9.cloned.1.call-update) | async-done | bytes 8388624 | tf_op jit(solution)/shard_map/all_gather | solution.py:17
  113.7 229.5 %all-gather.7.cloned.1.call-done = f32[1024,4096]{1,0:T(8,128)} async-done(((f32[1024,512]{1,0:T(8,128)}), f32[1024,4096]{1,0:T(8,128)}) %all-gather.7.cloned.1.call-update) | async-done | bytes 16777232 | tf_op jit(solution)/shard_map/all_gather | solution.py:16
  343.2 31.0 %fusion = f32[1024,512]{1,0:T(8,128)} fusion(f32[1024,4096]{1,0:T(8,128)} %all-gather.7.cloned.1.call-done, f32[4096,512]{1,0:T(8,128)} %all-gather.9.cloned.1.call-done), kind=kOutput, calls=%fused_computation.4 | convolution fusion | flops 25769803776 | bytes 27262976 | tf_op jit(solution)/shard_map/dot_general | solution.py:18
  374.2 0.0 all-gather.11.cloned.1.call-update
  374.2 0.2 all-gather.15.cloned.1.call-start
  374.5 56.4 %all-gather.11.cloned.1.call-done = f32[4096,512]{1,0:T(8,128)} async-done(((f32[1024,512]{1,0:T(8,128)}), f32[4096,512]{1,0:T(8,128)}) %all-gather.11.cloned.1.call-update) | async-done | bytes 8388624 | tf_op jit(solution)/shard_map/all_gather | solution.py:26
  430.8 31.2 %multiply_subtract_fusion.1 = f32[1024,512]{1,0:T(8,128)} fusion(f32[1024,512]{1,0:T(8,128)S(1)} %copy-done, f32[1024,4096]{1,0:T(8,128)} %all-gather.7.cloned.1.call-done, f32[4096,512]{1,0:T(8,128)} %all-gather.11.cloned.1.call-done), kind=kOutput, calls=%fused_computation.1 | convolution fusion | flops 25771376640 | bytes 29360128 | tf_op jit(solution)/shard_map/dot_general | solution.py:24
  462.1 0.0 all-gather.15.cloned.1.call-update
  462.1 0.0 all-gather.13.cloned.1.call-start
  462.1 0.5 all-gather.13.cloned.1.call-update
  462.7 0.3 all-gather.17.cloned.1.call-start
  463.0 57.6 %all-gather.15.cloned.1.call-done = f32[4096,512]{1,0:T(8,128)} async-done(((f32[1024,512]{1,0:T(8,128)}), f32[4096,512]{1,0:T(8,128)}) %all-gather.15.cloned.1.call-update) | async-done | bytes 8388624 | tf_op jit(solution)/shard_map/all_gather | solution.py:17
  520.5 229.3 %all-gather.13.cloned.1.call-done = f32[1024,4096]{1,0:T(8,128)} async-done(((f32[1024,512]{1,0:T(8,128)}), f32[1024,4096]{1,0:T(8,128)}) %all-gather.13.cloned.1.call-update) | async-done | bytes 16777232 | tf_op jit(solution)/shard_map/all_gather | solution.py:16
  749.8 31.0 %fusion.1 = f32[1024,512]{1,0:T(8,128)} fusion(f32[1024,4096]{1,0:T(8,128)} %all-gather.13.cloned.1.call-done, f32[4096,512]{1,0:T(8,128)} %all-gather.15.cloned.1.call-done), kind=kOutput, calls=%fused_computation.5 | convolution fusion | flops 25769803776 | bytes 27262976 | tf_op jit(solution)/shard_map/dot_general | solution.py:18
  780.9 0.0 all-gather.17.cloned.1.call-update
  780.9 56.6 %all-gather.17.cloned.1.call-done = f32[4096,512]{1,0:T(8,128)} async-done(((f32[1024,512]{1,0:T(8,128)}), f32[4096,512]{1,0:T(8,128)}) %all-gather.17.cloned.1.call-update) | async-done | bytes 8388624 | tf_op jit(solution)/shard_map/all_gather | solution.py:26
  837.5 31.2 %multiply_subtract_fusion = f32[1024,512]{1,0:T(8,128)} fusion(f32[1024,512]{1,0:T(8,128)S(1)} %copy-done.1, f32[1024,4096]{1,0:T(8,128)} %all-gather.13.cloned.1.call-done, f32[4096,512]{1,0:T(8,128)} %all-gather.17.cloned.1.call-done), kind=kOutput, calls=%fused_computation | convolution fusion | flops 25771376640 | bytes 29360128 | tf_op jit(solution)/shard_map/dot_general | solution.py:24
  (5 shorter events, 0.0 us)
Async XLA Ops:
  6.5 107.2 %all-gather.9.cloned.1.call-start = ((), (), s32[]{:S(2)}) async-start(), calls=%async_computation.1 | async-start | bytes 10485760 | tf_op jit(solution)/shard_map/all_gather | solution.py:17
  55.3 287.9 %all-gather.7.cloned.1.call-start = ((), (), s32[]{:S(2)}) async-start(), calls=%async_computation | async-start | bytes 18874368 | tf_op jit(solution)/shard_map/all_gather | solution.py:16
  56.1 374.8 %copy-start = (f32[1024,512]{1,0:T(8,128)S(1)}, f32[1024,512]{1,0:T(8,128)}, u32[]{:S(2)}) copy-start(f32[1024,512]{1,0:T(8,128)} %broadcast_multiply_fusion) | copy-start | bytes 6291460
  56.1 374.8 %all-gather.11.cloned.1.call-start = ((), (), s32[]{:S(2)}) async-start(), calls=%async_computation.2 | async-start | bytes 10485760 | tf_op jit(solution)/shard_map/all_gather | solution.py:26
  374.2 146.3 %all-gather.15.cloned.1.call-start = ((), (), s32[]{:S(2)}) async-start(), calls=%async_computation.4 | async-start | bytes 10485760 | tf_op jit(solution)/shard_map/all_gather | solution.py:17
  462.1 287.7 %all-gather.13.cloned.1.call-start = ((), (), s32[]{:S(2)}) async-start(), calls=%async_computation.3 | async-start | bytes 18874368 | tf_op jit(solution)/shard_map/all_gather | solution.py:16
  462.7 374.8 %copy-start.1 = (f32[1024,512]{1,0:T(8,128)S(1)}, f32[1024,512]{1,0:T(8,128)}, u32[]{:S(2)}) copy-start(f32[1024,512]{1,0:T(8,128)} %multiply_subtract_fusion.1) | copy-start | bytes 6291460
  462.7 374.8 %all-gather.17.cloned.1.call-start = ((), (), s32[]{:S(2)}) async-start(), calls=%async_computation.5 | async-start | bytes 10485760 | tf_op jit(solution)/shard_map/all_gather | solution.py:26
Sparse Core Ops, SparseCore 0:
  55.4 58.2 all-gather.8
  115.9 227.2 all-gather.6
  374.4 56.4 all-gather.10
  462.2 58.2 all-gather.14
  522.6 227.2 all-gather.12
  781.0 56.4 all-gather.16
where the time goes:
time: 876 us
  waiting for transfers between devices  688 us (79%)
  matrix products  125 us (14%)
  blocking collectives  42.2 us (5%)
  between operations  14.2 us (2%)
    all_gather x2, waiting for transfers between devices, shards(): rows_panel = lax.all_gather(source, 'col', axis=1, tiled=True)  459 us
    all_gather x2, waiting for transfers between devices, shards(): cols_panel = lax.all_gather(source, 'row', axis=0, tiled=True)  115 us
    all_gather x2, waiting for transfers between devices, shards(): lax.all_gather(square, 'row', axis=0, tiled=True)  113 us
    dot_general x2, matrix products, shards(): jnp.dot(rows_panel, lax.all_gather(square, 'row', axis=0, tiled=True), pr...  62.5 us
    dot_general x2, matrix products, shards(): jnp.dot(rows_panel, cols_panel, preferred_element_type=jnp.float32, preci...  62 us
    psum x1, blocking collectives, shards(): total = lax.psum(jnp.sum(matrix * matrix), ('row', 'col'))  42.2 us
  transfers between devices with their start and end apart: 6, of which 6 were waited for; matrix products, arithmetic and copies ran while one was open for 0% of the time, Pallas kernels for 0%

commit v1 on v0

--- a/solution.py
+++ b/solution.py
@@ -14,7 +14,14 @@
     for step in range(ITERS):
         source = x_iter
         rows_panel = lax.all_gather(source, "col", axis=1, tiled=True)
-        cols_panel = lax.all_gather(source, "row", axis=0, tiled=True)
+        size = lax.axis_size("row")
+        right = [(i, (i + 1) % size) for i in range(size)]
+        terms = [source]
+        for far in range(1, size):
+            terms = [lax.ppermute(terms[0], "row", right), *terms]
+        whole = jnp.concatenate(terms, axis=0)
+        places = (lax.axis_index("row") + 1) * terms[-1].shape[0]
+        cols_panel = jnp.roll(whole, places, axis=0)
         square = jnp.dot(
             rows_panel,
             cols_panel,

time: 876 us -> 768 us (0.88)
  waiting for transfers between devices: 688 us -> 563 us
  matrix products: 125 us -> 138 us
    all_gather x2, waiting for transfers between devices: 459 us -> 297 us  [shards(): rows_panel = lax.all_gather(source, 'col', axis=1, tiled=True)]
    ppermute x0 -> x6, waiting for transfers between devices: none -> 153 us  [shards(): terms = [lax.ppermute(terms[0], 'row', right), *terms]]
    all_gather x2 -> x0, waiting for transfers between devices: 115 us -> none  [shards(): cols_panel = lax.all_gather(source, 'row', axis=0, tiled=True)]
    dot_general x2, matrix products: 62 us -> 75.5 us  [shards(): jnp.dot(rows_panel, cols_panel, preferred_element_type=jnp.float32, preci...]
  transfers between devices with their start and end apart: 6 -> 10, of which waited for: 6 -> 10; matrix products, arithmetic and copies ran while one was open for 0% -> 0% of each run, Pallas kernels for 0% -> 0%
where the time goes in v1:
time: 768 us
  waiting for transfers between devices  563 us (73%)
  matrix products  138 us (18%)
  blocking collectives  42.2 us (5%)
  between operations  13.9 us (2%)
    all_gather x2, waiting for transfers between devices, shards(): rows_panel = lax.all_gather(source, 'col', axis=1, tiled=True)  297 us
    ppermute x6, waiting for transfers between devices, shards(): terms = [lax.ppermute(terms[0], 'row', right), *terms]  153 us
    all_gather x2, waiting for transfers between devices, shards(): lax.all_gather(square, 'row', axis=0, tiled=True)  113 us
    dot_general x2, matrix products, shards(): jnp.dot(rows_panel, cols_panel, preferred_element_type=jnp.float32, preci...  75.5 us
    dot_general x2, matrix products, shards(): jnp.dot(rows_panel, lax.all_gather(square, 'row', axis=0, tiled=True), pr...  62.5 us
    psum x1, blocking collectives, shards(): total = lax.psum(jnp.sum(matrix * matrix), ('row', 'col'))  42.2 us
  transfers between devices with their start and end apart: 10, of which 10 were waited for; matrix products, arithmetic and copies ran while one was open for 0% of the time, Pallas kernels for 0%

profile of v1, /device:TPU:0, one launch (start us, length us, event | category | flops | bytes accessed | tf_op | source)
XLA Modules:
  0.0 768.0 jit_solution(5348244995914458045)
XLA Ops:
  6.5 2.7 multiply_reduce_fusion
  9.3 42.2 %psum.7 = f32[]{:T(128)} all-reduce(f32[]{:T(128)} %multiply_reduce_fusion), channel_id=1, replica_groups=mesh['row'=4,'col'=8] {'row','col'}, use_global_device_ids=true, to_apply=%region_1.0 | all-reduce | flops 1 | bytes 8 | tf_op jit(solution)/shard_map/psum | solution.py:11
  52.2 3.1 broadcast_multiply_fusion
  55.4 0.1 collective-permute-start
  55.4 25.7 %collective-permute-done = f32[1024,512]{1,0:T(8,128)S(1)} collective-permute-done((f32[1024,512]{1,0:T(8,128)}, f32[1024,512]{1,0:T(8,128)S(1)}, u32[]{:S(2)}, u32[]{:S(2)}) %collective-permute-start) | collective-permute-done | bytes 2097184 | tf_op jit(solution)/shard_map/ppermute | solution.py:21
  81.1 1.3 copy-done.2
  82.4 0.2 collective-permute-start.1
  82.7 25.4 %collective-permute-done.1 = f32[1024,512]{1,0:T(8,128)} collective-permute-done((f32[1024,512]{1,0:T(8,128)S(1)}, f32[1024,512]{1,0:T(8,128)}, u32[]{:S(2)}, u32[]{:S(2)}) %collective-permute-start.1) | collective-permute-done | bytes 2097184 | tf_op jit(solution)/shard_map/ppermute | solution.py:21
  108.0 25.8 %collective-permute-done.2 = f32[1024,512]{1,0:T(8,128)} collective-permute-done((f32[1024,512]{1,0:T(8,128)}, f32[1024,512]{1,0:T(8,128)}, u32[]{:S(2)}, u32[]{:S(2)}) %collective-permute-start.2) | collective-permute-done | bytes 2097184 | tf_op jit(solution)/shard_map/ppermute | solution.py:21
  133.8 148.9 %all-gather.5.cloned.1.call-done = f32[1024,4096]{1,0:T(8,128)} async-done(((f32[1024,512]{1,0:T(8,128)}), f32[1024,4096]{1,0:T(8,128)}) %all-gather.5.cloned.1.call-update) | async-done | bytes 16777232 | tf_op jit(solution)/shard_map/all_gather | solution.py:16
  282.7 37.8 %fusion.14 = f32[1024,512]{1,0:T(8,128)} fusion(f32[1024,4096]{1,0:T(8,128)} %all-gather.5.cloned.1.call-done, s32[]{:T(128)S(6)} %select_n.13, f32[1024,512]{1,0:T(8,128)} %collective-permute-done.2, f32[1024,512]{1,0:T(8,128)} %collective-permute-done.1, f32[1024,512]{1,0:T(8,128)} %copy-done.2, f32[1024,512]{1,0:T(8,128)} %broadcast_multiply_fusion), kind=kOutput, calls=%fused_computation.28 | convolution fusion | flops 25784483840 | bytes 27262980 | tf_op jit(solution)/shard_map/dot_general | solution.py:25
  320.5 0.2 all-gather.9.cloned.1.call-start
  320.7 56.4 %all-gather.7.cloned.1.call-done = f32[4096,512]{1,0:T(8,128)} async-done(((f32[1024,512]{1,0:T(8,128)}), f32[4096,512]{1,0:T(8,128)}) %all-gather.7.cloned.1.call-update) | async-done | bytes 8388624 | tf_op jit(solution)/shard_map/all_gather | solution.py:33
  377.1 31.2 %multiply_subtract_fusion.1 = f32[1024,512]{1,0:T(8,128)} fusion(f32[1024,512]{1,0:T(8,128)S(1)} %copy-done, f32[1024,4096]{1,0:T(8,128)} %all-gather.5.cloned.1.call-done, f32[4096,512]{1,0:T(8,128)} %all-gather.7.cloned.1.call-done), kind=kOutput, calls=%fused_computation.33 | convolution fusion | flops 25771376640 | bytes 29360128 | tf_op jit(solution)/shard_map/dot_general | solution.py:31
  408.4 0.3 collective-permute-start.3
  408.7 25.4 %collective-permute-done.3 = f32[1024,512]{1,0:T(8,128)S(1)} collective-permute-done((f32[1024,512]{1,0:T(8,128)}, f32[1024,512]{1,0:T(8,128)S(1)}, u32[]{:S(2)}, u32[]{:S(2)}) %collective-permute-start.3) | collective-permute-done | bytes 2097184 | tf_op jit(solution)/shard_map/ppermute | solution.py:21
  434.2 1.3 copy-done.3
  435.5 25.5 %collective-permute-done.4 = f32[1024,512]{1,0:T(8,128)S(1)} collective-permute-done((f32[1024,512]{1,0:T(8,128)S(1)}, f32[1024,512]{1,0:T(8,128)S(1)}, u32[]{:S(2)}, u32[]{:S(2)}) %collective-permute-start.4) | collective-permute-done | bytes 2097184 | tf_op jit(solution)/shard_map/ppermute | solution.py:21
  461.0 1.3 copy-done.4
  462.3 25.6 %collective-permute-done.5 = f32[1024,512]{1,0:T(8,128)} collective-permute-done((f32[1024,512]{1,0:T(8,128)S(1)}, f32[1024,512]{1,0:T(8,128)}, u32[]{:S(2)}, u32[]{:S(2)}) %collective-permute-start.5) | collective-permute-done | bytes 2097184 | tf_op jit(solution)/shard_map/ppermute | solution.py:21
  487.9 147.9 %all-gather.9.cloned.1.call-done = f32[1024,4096]{1,0:T(8,128)} async-done(((f32[1024,512]{1,0:T(8,128)}), f32[1024,4096]{1,0:T(8,128)}) %all-gather.9.cloned.1.call-update) | async-done | bytes 16777232 | tf_op jit(solution)/shard_map/all_gather | solution.py:16
  635.8 37.8 %fusion.4 = f32[1024,512]{1,0:T(8,128)} fusion(f32[1024,4096]{1,0:T(8,128)} %all-gather.9.cloned.1.call-done, s32[]{:T(128)S(6)} %select_n.13, f32[1024,512]{1,0:T(8,128)} %collective-permute-done.5, f32[1024,512]{1,0:T(8,128)} %copy-done.4, f32[1024,512]{1,0:T(8,128)} %copy-done.3, f32[1024,512]{1,0:T(8,128)} %multiply_subtract_fusion.1), kind=kOutput, calls=%fused_computation.20 | convolution fusion | flops 25784483840 | bytes 27262980 | tf_op jit(solution)/shard_map/dot_general | solution.py:25
  673.6 56.6 %all-gather.11.cloned.1.call-done = f32[4096,512]{1,0:T(8,128)} async-done(((f32[1024,512]{1,0:T(8,128)}), f32[4096,512]{1,0:T(8,128)}) %all-gather.11.cloned.1.call-update) | async-done | bytes 8388624 | tf_op jit(solution)/shard_map/all_gather | solution.py:33
  730.2 31.2 %multiply_subtract_fusion = f32[1024,512]{1,0:T(8,128)} fusion(f32[1024,512]{1,0:T(8,128)S(1)} %copy-done.1, f32[1024,4096]{1,0:T(8,128)} %all-gather.9.cloned.1.call-done, f32[4096,512]{1,0:T(8,128)} %all-gather.11.cloned.1.call-done), kind=kOutput, calls=%fused_computation.32 | convolution fusion | flops 25771376640 | bytes 29360128 | tf_op jit(solution)/shard_map/dot_general | solution.py:31
  (17 shorter events, 0.2 us)
Async XLA Ops:
  6.5 276.2 %all-gather.5.cloned.1.call-start = ((), (), s32[]{:S(2)}) async-start(), calls=%async_computation | async-start | bytes 18874368 | tf_op jit(solution)/shard_map/all_gather | solution.py:16
  55.3 321.8 %all-gather.7.cloned.1.call-start = ((), (), s32[]{:S(2)}) async-start(), calls=%async_computation.1 | async-start | bytes 10485760 | tf_op jit(solution)/shard_map/all_gather | solution.py:33
  55.4 25.7 %collective-permute-start = (f32[1024,512]{1,0:T(8,128)}, f32[1024,512]{1,0:T(8,128)S(1)}, u32[]{:S(2)}, u32[]{:S(2)}) collective-permute-start(f32[1024,512]{1,0:T(8,128)} %broadcast_multiply_fusion), channel_id=1, source_target_pairs={{0,8},{8,16},{16,24},{24,0},{1,9},{9,17},{17,25},{25,1},{2,10},{10... | collective-permute-start | bytes 6291464 | tf_op jit(solution)/shard_map/ppermute | solution.py:21
  81.1 1.3 copy-start.2
  82.4 25.6 %collective-permute-start.1 = (f32[1024,512]{1,0:T(8,128)S(1)}, f32[1024,512]{1,0:T(8,128)}, u32[]{:S(2)}, u32[]{:S(2)}) collective-permute-start(f32[1024,512]{1,0:T(8,128)S(1)} %collective-permute-done), channel_id=1, source_target_pairs={{0,8},{8,16},{16,24},{24,0},{1,9},{9,17},{17,25},{25,1},{2,10},{10... | collective-permute-start | bytes 6291464 | tf_op jit(solution)/shard_map/ppermute | solution.py:21
  108.0 25.8 %collective-permute-start.2 = (f32[1024,512]{1,0:T(8,128)}, f32[1024,512]{1,0:T(8,128)}, u32[]{:S(2)}, u32[]{:S(2)}) collective-permute-start(f32[1024,512]{1,0:T(8,128)} %collective-permute-done.1), channel_id=1, source_target_pairs={{0,8},{8,16},{16,24},{24,0},{1,9},{9,17},{17,25},{25,1},{2,10},{10... | collective-permute-start | bytes 6291464 | tf_op jit(solution)/shard_map/ppermute | solution.py:21
  108.0 269.1 %copy-start = (f32[1024,512]{1,0:T(8,128)S(1)}, f32[1024,512]{1,0:T(8,128)}, u32[]{:S(2)}) copy-start(f32[1024,512]{1,0:T(8,128)} %broadcast_multiply_fusion) | copy-start | bytes 6291460
  320.5 315.3 %all-gather.9.cloned.1.call-start = ((), (), s32[]{:S(2)}) async-start(), calls=%async_computation.2 | async-start | bytes 18874368 | tf_op jit(solution)/shard_map/all_gather | solution.py:16
  408.4 321.8 %copy-start.1 = (f32[1024,512]{1,0:T(8,128)S(1)}, f32[1024,512]{1,0:T(8,128)}, u32[]{:S(2)}) copy-start(f32[1024,512]{1,0:T(8,128)} %multiply_subtract_fusion.1) | copy-start | bytes 6291460
  408.4 321.8 %all-gather.11.cloned.1.call-start = ((), (), s32[]{:S(2)}) async-start(), calls=%async_computation.3 | async-start | bytes 10485760 | tf_op jit(solution)/shard_map/all_gather | solution.py:33
  408.4 25.7 %collective-permute-start.3 = (f32[1024,512]{1,0:T(8,128)}, f32[1024,512]{1,0:T(8,128)S(1)}, u32[]{:S(2)}, u32[]{:S(2)}) collective-permute-start(f32[1024,512]{1,0:T(8,128)} %multiply_subtract_fusion.1), channel_id=1, source_target_pairs={{0,8},{8,16},{16,24},{24,0},{1,9},{9,17},{17,25},{25,1},{2,10},{10... | collective-permute-start | bytes 6291464 | tf_op jit(solution)/shard_map/ppermute | solution.py:21
  434.2 1.3 copy-start.3
  435.5 25.5 %collective-permute-start.4 = (f32[1024,512]{1,0:T(8,128)S(1)}, f32[1024,512]{1,0:T(8,128)S(1)}, u32[]{:S(2)}, u32[]{:S(2)}) collective-permute-start(f32[1024,512]{1,0:T(8,128)S(1)} %collective-permute-done.3), channel_id=1, source_target_pairs={{0,8},{8,16},{16,24},{24,0},{1,9},{9,17},{17,25},{25,1},{2,10},{10... | collective-permute-start | bytes 6291464 | tf_op jit(solution)/shard_map/ppermute | solution.py:21
  461.0 1.3 copy-start.4
  462.3 25.6 %collective-permute-start.5 = (f32[1024,512]{1,0:T(8,128)S(1)}, f32[1024,512]{1,0:T(8,128)}, u32[]{:S(2)}, u32[]{:S(2)}) collective-permute-start(f32[1024,512]{1,0:T(8,128)S(1)} %collective-permute-done.4), channel_id=1, source_target_pairs={{0,8},{8,16},{16,24},{24,0},{1,9},{9,17},{17,25},{25,1},{2,10},{10... | collective-permute-start | bytes 6291464 | tf_op jit(solution)/shard_map/ppermute | solution.py:21
Sparse Core Ops, SparseCore 0:
  55.4 227.2 all-gather.4
  320.6 56.4 all-gather.6
  408.5 227.2 all-gather.8
  673.7 56.4 all-gather.10
